TPU v7x, 32 devices: a whole 2x2x4 slice. The times are simulated.
32 devices in a mesh: seq: 2 (over core), row: 4 (over z), col: 4 (over y, x).
Axes of the slice: x: 2, y: 2, z: 4, core: 2. Of those that a mesh axis runs over, the one named last changes fastest.
Arguments:
- alignment: bfloat16 [128, 32, 256], P('seq', ('row', 'col')), may hold values from -6 to 6, as said below
- row_mask: int32 [128, 32], P('seq', ('row', 'col')), may hold values 0 or 1
- norm_gain: float32 [256], replicated, may hold values from 0.5 to 1.5
- norm_bias: float32 [256], replicated, may hold values from -1.5 to 1.5
- left_weight: bfloat16 [256, 32], replicated, may hold values from -0.375 to 0.375
- left_bias: float32 [32], replicated, may hold values from -6 to 6
- right_weight: bfloat16 [256, 32], replicated, may hold values from -0.375 to 0.375
- right_bias: float32 [32], replicated, may hold values from -6 to 6
- pair_weight: float32 [1024, 128], replicated, may hold values from -0.375 to 0.375
- pair_state: bfloat16 [32, 32, 128], P('row', 'col'), may hold values from -6 to 6
Outputs:
- new_pair: bfloat16 [32, 32, 128], P('row', 'col')
Inputs may be any that keep to these rules, and one draw needn't show every extreme that they name: alignment rows come in 8 clusters of consecutive rows that share a profile per residue, entries within -6 to 6.
All inputs are finite; a program needn't handle non-finite values.
Results may differ from a plain program's by a relative error of at most 0.001.
Values may be sent and summed in bfloat16 or wider, within the bound.
A program may use at most 64 MiB of HBM per device.

v0:
```python
import jax
import jax.numpy as jnp
from jax import lax
from jax.sharding import PartitionSpec as P

variance_floor = 1e-05
count_floor = 0.001


def layer_norm(alignment, norm_gain, norm_bias):
    values = alignment.astype(jnp.float32)
    center = jnp.mean(values, axis=-1, keepdims=True)
    spread = jnp.mean((values - center) ** 2, axis=-1, keepdims=True)
    return ((values - center) * lax.rsqrt(spread + variance_floor) * norm_gain + norm_bias).astype(
        jnp.bfloat16
    )


def project(normed, weight, offset, mask_float, marker):
    result = (
        (jnp.dot(normed, weight, preferred_element_type=jnp.float32) + offset)
        * mask_float[:, :, None]
    ).astype(jnp.bfloat16)
    return jnp.concatenate([result, marker], axis=-1)


def outer_block(left_part, right_part):
    depth, left_count, width = left_part.shape
    right_count = right_part.shape[1]
    product = lax.dot_general(
        left_part.reshape(depth, left_count * width),
        right_part.reshape(depth, right_count * width),
        (((0,), (0,)), ((), ())),
        preferred_element_type=jnp.float32,
    )
    return product.reshape(left_count, width, right_count, width).transpose(0, 2, 1, 3)


def split_joint(joint):
    channels = joint.shape[-1] - 1
    flat_sums = joint[:, :, :channels, :channels].reshape(
        joint.shape[0], joint.shape[1], channels * channels
    )
    count_sums = joint[:, :, channels, channels]
    return (flat_sums, count_sums)


def finish(flat_sums, count_sums, pair_rows, pair_weight):
    update = (
        jnp.dot(flat_sums, pair_weight, precision=lax.Precision.HIGHEST)
        / (count_floor + count_sums)[:, :, None]
    )
    return (pair_rows.astype(jnp.float32) + update).astype(jnp.bfloat16)


def column_block(whole_right):
    block_width = whole_right.shape[1] // lax.axis_size("col")
    return lax.dynamic_slice_in_dim(
        whole_right, lax.axis_index("col") * block_width, block_width, 1
    )


def on_device(
    alignment,
    row_mask,
    norm_gain,
    norm_bias,
    left_weight,
    left_bias,
    right_weight,
    right_bias,
    pair_weight,
    pair_state,
):
    normed = layer_norm(alignment, norm_gain, norm_bias)
    mask_float = row_mask.astype(jnp.float32)
    marker = mask_float.astype(jnp.bfloat16)[:, :, None]
    left = project(normed, left_weight, left_bias, mask_float, marker)
    right = project(normed, right_weight, right_bias, mask_float, marker)
    rows_left, rows_right = (
        lax.all_gather(left, "col", axis=1, tiled=True),
        lax.all_gather(right, "col", axis=1, tiled=True),
    )
    deep_left, deep_right = (
        lax.all_gather(rows_left, "seq", axis=0, tiled=True),
        lax.all_gather(rows_right, "seq", axis=0, tiled=True),
    )
    whole_right = lax.all_gather(deep_right, "row", axis=1, tiled=True)
    joint = outer_block(deep_left, column_block(whole_right))
    flat_sums, count_sums = split_joint(joint)
    return finish(flat_sums, count_sums, pair_state, pair_weight)


def solution(mesh):
    placed = (
        P("seq", ("row", "col"), None),
        P("seq", ("row", "col")),
        P(),
        P(),
        P(),
        P(),
        P(),
        P(),
        P(),
        P("row", "col", None),
    )
    return jax.shard_map(
        on_device, mesh=mesh, in_specs=placed, out_specs=P("row", "col", None), check_vma=False
    )
```

profile of v0, /device:TPU:0, one launch (start us, length us, event | category | flops | bytes accessed | tf_op | source)
XLA Modules:
  0.0 44.4 jit_solution(13767113097260525965)
XLA Ops:
  0.0 0.0 copy-start
  0.0 0.7 %fusion.19 = (f32[64,2]{0,1:T(2,128)S(1)}, bf16[64,2,1]{0,1,2:T(2,128)(2,1)S(1)}) fusion(s32[64,2]{0,1:T(2,128)} %param.11), kind=kLoop, calls=%fused_computation.32 | loop fusion | flops 256 | bytes 1280 | tf_op jit(solution)/shard_map/convert_element_type | solution.py:76
  0.8 1.0 %convert_reduce_fusion = f32[64,2]{1,0:T(8,128)S(1)} fusion(bf16[64,2,256]{2,1,0:T(2,128)(2,1)} %param.10), kind=kLoop, calls=%fused_computation.12 | loop fusion | flops 65408 | bytes 66048 | tf_op jit(solution)/shard_map/reduce_sum | solution.py:12
  1.8 1.1 %fusion.9 = f32[64,2]{1,0:T(8,128)S(1)} fusion(bf16[64,2,256]{2,1,0:T(2,128)(2,1)} %param.10, f32[64,2]{1,0:T(8,128)S(1)} %broadcast_multiply_fusion), kind=kLoop, calls=%fused_computation.15 | loop fusion | flops 130944 | bytes 66560 | tf_op jit(solution)/shard_map/reduce_sum | solution.py:13
  2.8 1.1 %fusion.12 = bf16[64,2,256]{2,1,0:T(2,128)(2,1)S(1)} fusion(bf16[64,2,256]{2,1,0:T(2,128)(2,1)} %param.10, f32[256]{0:T(256)} %param.13, f32[256]{0:T(256)} %param.12, f32[64,2]{1,0:T(8,128)S(1)} %add_rsqrt_fusion, f32[64,2]{1,0:T(8,128)S(1)} %broadcast_multiply_fusion), kind=kLoop, calls=%fused_computation.18 | loop fusion | flops 196608 | bytes 134144 | tf_op jit(solution)/shard_map/convert_element_type | solution.py:14
  3.9 0.8 %fusion.4 = bf16[64,2,32]{0,2,1:T(8,128)(2,1)S(1)} fusion(bf16[64,2,256]{2,1,0:T(2,128)(2,1)S(1)} %fusion.12, bf16[256,32]{0,1:T(8,128)(2,1)} %param.16, f32[32]{0:T(128)} %param.17, f32[64,2]{0,1:T(2,128)S(1)} %get-tuple-element.7), kind=kOutput, calls=%fused_computation.8 | convolution fusion | flops 2109440 | bytes 90752 | tf_op jit(solution)/shard_map/dot_general | solution.py:21
  4.8 0.9 %fusion.3 = bf16[64,2,32]{0,2,1:T(8,128)(2,1)S(1)} fusion(bf16[64,2,256]{2,1,0:T(2,128)(2,1)S(1)} %fusion.12, bf16[256,32]{0,1:T(8,128)(2,1)} %param.14, f32[64,2]{0,1:T(2,128)S(1)} %get-tuple-element.7, f32[32]{0:T(128)} %param.15), kind=kOutput, calls=%fused_computation.7 | convolution fusion | flops 2109440 | bytes 90752 | tf_op jit(solution)/shard_map/dot_general | solution.py:21
  5.7 0.1 pad_maximum_fusion.1
  5.7 9.8 %all_gather.15 = bf16[64,8,33]{0,2,1:T(8,128)(2,1)S(1)} all-gather(bf16[64,2,33]{0,2,1:T(8,128)(2,1)S(1)} %get-tuple-element.5), channel_id=1, replica_groups=mesh['seq'=2,'row'=4,'col'=4] {'col'}, dimensions={1}, use_global_device_ids=true | all-gather | bytes 42240 | tf_op jit(solution)/shard_map/all_gather | solution.py:81
  15.6 0.2 copy.21
  15.7 8.3 %all_gather.17 = bf16[64,8,33]{0,2,1:T(8,128)(2,1)S(1)} all-gather(bf16[64,2,33]{0,2,1:T(8,128)(2,1)S(1)} %get-tuple-element.6), channel_id=1, replica_groups=mesh['seq'=2,'row'=4,'col'=4] {'col'}, dimensions={1}, use_global_device_ids=true | all-gather | bytes 42240 | tf_op jit(solution)/shard_map/all_gather | solution.py:82
  24.1 0.2 copy.25
  24.2 2.0 %all_gather.18 = bf16[128,8,33]{2,1,0:T(8,128)(2,1)S(1)} all-gather(bf16[64,8,33]{2,1,0:T(8,128)(2,1)S(1)} %copy.25), channel_id=1, replica_groups=mesh['seq'=2,'row'=4,'col'=4] {'seq'}, dimensions={0}, use_global_device_ids=true | all-gather | bytes 101376 | tf_op jit(solution)/shard_map/all_gather | solution.py:86
  26.2 0.2 copy.26
  26.4 2.0 %all_gather.16 = bf16[128,8,33]{2,1,0:T(8,128)(2,1)S(1)} all-gather(bf16[64,8,33]{2,1,0:T(8,128)(2,1)S(1)} %copy.21), channel_id=1, replica_groups=mesh['seq'=2,'row'=4,'col'=4] {'seq'}, dimensions={0}, use_global_device_ids=true | all-gather | bytes 101376 | tf_op jit(solution)/shard_map/all_gather | solution.py:85
  28.4 0.2 reshape.44
  28.6 0.1 copy.29
  28.8 13.0 %all_gather.19 = bf16[128,32,33]{0,1,2:T(8,128)(2,1)S(1)} all-gather(bf16[128,8,33]{0,1,2:T(8,128)(2,1)S(1)} %copy.26), channel_id=1, replica_groups=mesh['seq'=2,'row'=4,'col'=4] {'row'}, dimensions={1}, use_global_device_ids=true | all-gather | bytes 337920 | tf_op jit(solution)/shard_map/all_gather | solution.py:88
  42.0 0.3 convolution_bitcast_fusion
  42.3 0.3 fusion.16
  42.6 0.0 copy-start.1
  42.6 0.1 slice.8
  42.7 0.5 %reshape.38 = f32[8,8,1024]{2,1,0:T(8,128)S(1)} reshape(f32[8,8,32,32]{3,2,1,0:T(8,128)S(1)} %slice.8) | data formatting | bytes 524288 | tf_op jit(solution)/shard_map/reshape | solution.py:41
  43.2 0.0 copy-done
  43.2 0.1 copy-done.1
  43.3 1.1 %fusion.5 = bf16[8,8,128]{2,1,0:T(8,128)(2,1)} fusion(f32[8,8,1024]{2,1,0:T(8,128)S(1)} %reshape.38, f32[1024,128]{1,0:T(8,128)S(1)} %copy-done, bf16[8,8,128]{2,1,0:T(8,128)(2,1)S(1)} %copy-done.1, f32[8,8]{1,0:T(8,128)S(1)} %fusion.16), kind=kOutput, calls=%fused_computation.9 | convolution fusion | flops 100696064 | bytes 819456 | tf_op jit(solution)/shard_map/dot_general | solution.py:50
  (8 shorter events, 0.2 us)
Async XLA Ops:
  0.0 43.2 %copy-start = (f32[1024,128]{1,0:T(8,128)S(1)}, f32[1024,128]{1,0:T(8,128)}, u32[]{:S(2)}) copy-start(f32[1024,128]{1,0:T(8,128)} %param.18) | copy-start | bytes 1572868
  42.6 0.7 %copy-start.1 = (bf16[8,8,128]{2,1,0:T(8,128)(2,1)S(1)}, bf16[8,8,128]{2,1,0:T(8,128)(2,1)}, u32[]{:S(2)}) copy-start(bf16[8,8,128]{2,1,0:T(8,128)(2,1)} %param.19) | copy-start | bytes 49156
where the time goes:
time: 44.8 us; the launch traced here: 44.4 us
  blocking collectives  35.2 us (79%)
  other arithmetic  4.18 us (9%)
  matrix products  3.14 us (7%)
  local copies, waits for them, and re-layouts  1.69 us (4%)
    all_gather x1, blocking collectives, on_device(): whole_right = lax.all_gather(deep_right, 'row', axis=1, tiled=True)  13 us
    all_gather x1, blocking collectives, on_device(): lax.all_gather(left, 'col', axis=1, tiled=True)  9.84 us
    all_gather x1, blocking collectives, on_device(): lax.all_gather(right, 'col', axis=1, tiled=True)  8.33 us
    all_gather x1, blocking collectives, on_device(): lax.all_gather(rows_right, 'seq', axis=0, tiled=True)  1.99 us
    all_gather x1, blocking collectives, on_device(): lax.all_gather(rows_left, 'seq', axis=0, tiled=True)  1.99 us
    dot_general x2, matrix products, project(): jnp.dot(normed, weight, preferred_element_type=jnp.float32) + offset  1.73 us
    reduce_sum x1, other arithmetic, layer_norm(): spread = jnp.mean((values - center) ** 2, axis=-1, keepdims=True)  1.06 us
    convert_element_type x1, other arithmetic, layer_norm(): ((values - center) * lax.rsqrt(spread + variance_floor) * norm_gain + nor...  1.06 us

commit v1 on v0

--- a/solution.py
+++ b/solution.py
@@ -85,7 +85,7 @@
         lax.all_gather(rows_left, "seq", axis=0, tiled=True),
         lax.all_gather(rows_right, "seq", axis=0, tiled=True),
     )
-    whole_right = lax.all_gather(deep_right, "row", axis=1, tiled=True)
+    whole_right = jnp.concatenate(lax.all_gather(deep_right, "row"), axis=1)
     joint = outer_block(deep_left, column_block(whole_right))
     flat_sums, count_sums = split_joint(joint)
     return finish(flat_sums, count_sums, pair_state, pair_weight)

time: 44.8 us -> 45 us (level)
  no operation moved by 1% of the time
where the time goes in v1:
time: 45 us; the launch traced here: 44.5 us
  blocking collectives  35.2 us (78%)
  other arithmetic  4.18 us (9%)
  matrix products  3.14 us (7%)
  local copies, waits for them, and re-layouts  1.81 us (4%)
    all_gather x1, blocking collectives, on_device(): whole_right = jnp.concatenate(lax.all_gather(deep_right, 'row'), axis=1)  13 us
    all_gather x1, blocking collectives, on_device(): lax.all_gather(left, 'col', axis=1, tiled=True)  9.84 us
    all_gather x1, blocking collectives, on_device(): lax.all_gather(right, 'col', axis=1, tiled=True)  8.33 us
    all_gather x1, blocking collectives, on_device(): lax.all_gather(rows_right, 'seq', axis=0, tiled=True)  1.99 us
    all_gather x1, blocking collectives, on_device(): lax.all_gather(rows_left, 'seq', axis=0, tiled=True)  1.99 us
    dot_general x2, matrix products, project(): jnp.dot(normed, weight, preferred_element_type=jnp.float32) + offset  1.73 us
    reduce_sum x1, other arithmetic, layer_norm(): spread = jnp.mean((values - center) ** 2, axis=-1, keepdims=True)  1.06 us
    convert_element_type x1, other arithmetic, layer_norm(): ((values - center) * lax.rsqrt(spread + variance_floor) * norm_gain + nor...  1.06 us

profile of v1, /device:TPU:0, one launch (start us, length us, event | category | flops | bytes accessed | tf_op | source)
XLA Modules:
  0.0 44.5 jit_solution(13932327713554181195)
XLA Ops:
  0.0 0.0 copy-start
  0.0 0.7 %fusion.19 = (f32[64,2]{0,1:T(2,128)S(1)}, bf16[64,2,1]{0,1,2:T(2,128)(2,1)S(1)}) fusion(s32[64,2]{0,1:T(2,128)} %param.11), kind=kLoop, calls=%fused_computation.33 | loop fusion | flops 256 | bytes 1280 | tf_op jit(solution)/shard_map/convert_element_type | solution.py:76
  0.8 1.0 %convert_reduce_fusion = f32[64,2]{1,0:T(8,128)S(1)} fusion(bf16[64,2,256]{2,1,0:T(2,128)(2,1)} %param.10), kind=kLoop, calls=%fused_computation.13 | loop fusion | flops 65408 | bytes 66048 | tf_op jit(solution)/shard_map/reduce_sum | solution.py:12
  1.8 1.1 %fusion.9 = f32[64,2]{1,0:T(8,128)S(1)} fusion(bf16[64,2,256]{2,1,0:T(2,128)(2,1)} %param.10, f32[64,2]{1,0:T(8,128)S(1)} %broadcast_multiply_fusion), kind=kLoop, calls=%fused_computation.16 | loop fusion | flops 130944 | bytes 66560 | tf_op jit(solution)/shard_map/reduce_sum | solution.py:13
  2.8 1.1 %fusion.12 = bf16[64,2,256]{2,1,0:T(2,128)(2,1)S(1)} fusion(bf16[64,2,256]{2,1,0:T(2,128)(2,1)} %param.10, f32[256]{0:T(256)} %param.13, f32[256]{0:T(256)} %param.12, f32[64,2]{1,0:T(8,128)S(1)} %add_rsqrt_fusion, f32[64,2]{1,0:T(8,128)S(1)} %broadcast_multiply_fusion), kind=kLoop, calls=%fused_computation.19 | loop fusion | flops 196608 | bytes 134144 | tf_op jit(solution)/shard_map/convert_element_type | solution.py:14
  3.9 0.8 %fusion.4 = bf16[64,2,32]{0,2,1:T(8,128)(2,1)S(1)} fusion(bf16[64,2,256]{2,1,0:T(2,128)(2,1)S(1)} %fusion.12, bf16[256,32]{0,1:T(8,128)(2,1)} %param.16, f32[32]{0:T(128)} %param.17, f32[64,2]{0,1:T(2,128)S(1)} %get-tuple-element.7), kind=kOutput, calls=%fused_computation.8 | convolution fusion | flops 2109440 | bytes 90752 | tf_op jit(solution)/shard_map/dot_general | solution.py:21
  4.8 0.9 %fusion.3 = bf16[64,2,32]{0,2,1:T(8,128)(2,1)S(1)} fusion(bf16[64,2,256]{2,1,0:T(2,128)(2,1)S(1)} %fusion.12, bf16[256,32]{0,1:T(8,128)(2,1)} %param.14, f32[64,2]{0,1:T(2,128)S(1)} %get-tuple-element.7, f32[32]{0:T(128)} %param.15), kind=kOutput, calls=%fused_computation.7 | convolution fusion | flops 2109440 | bytes 90752 | tf_op jit(solution)/shard_map/dot_general | solution.py:21
  5.7 0.1 pad_maximum_fusion.1
  5.7 9.8 %all_gather.18 = bf16[64,8,33]{0,2,1:T(8,128)(2,1)S(1)} all-gather(bf16[64,2,33]{0,2,1:T(8,128)(2,1)S(1)} %get-tuple-element.5), channel_id=1, replica_groups=mesh['seq'=2,'row'=4,'col'=4] {'col'}, dimensions={1}, use_global_device_ids=true | all-gather | bytes 42240 | tf_op jit(solution)/shard_map/all_gather | solution.py:81
  15.6 0.2 copy.34
  15.7 8.3 %all_gather.20 = bf16[64,8,33]{0,2,1:T(8,128)(2,1)S(1)} all-gather(bf16[64,2,33]{0,2,1:T(8,128)(2,1)S(1)} %get-tuple-element.6), channel_id=1, replica_groups=mesh['seq'=2,'row'=4,'col'=4] {'col'}, dimensions={1}, use_global_device_ids=true | all-gather | bytes 42240 | tf_op jit(solution)/shard_map/all_gather | solution.py:82
  24.1 0.2 copy.38
  24.2 2.0 %all_gather.21 = bf16[128,8,33]{2,1,0:T(8,128)(2,1)S(1)} all-gather(bf16[64,8,33]{2,1,0:T(8,128)(2,1)S(1)} %copy.38), channel_id=1, replica_groups=mesh['seq'=2,'row'=4,'col'=4] {'seq'}, dimensions={0}, use_global_device_ids=true | all-gather | bytes 101376 | tf_op jit(solution)/shard_map/all_gather | solution.py:86
  26.2 0.2 copy.39
  26.4 2.0 %all_gather.19 = bf16[128,8,33]{2,1,0:T(8,128)(2,1)S(1)} all-gather(bf16[64,8,33]{2,1,0:T(8,128)(2,1)S(1)} %copy.34), channel_id=1, replica_groups=mesh['seq'=2,'row'=4,'col'=4] {'seq'}, dimensions={0}, use_global_device_ids=true | all-gather | bytes 101376 | tf_op jit(solution)/shard_map/all_gather | solution.py:85
  28.4 0.2 reshape.53
  28.6 0.1 copy.43
  28.8 13.0 %all-gather = bf16[512,8,33]{0,1,2:T(8,128)(2,1)S(1)} all-gather(bf16[128,8,33]{0,1,2:T(8,128)(2,1)S(1)} %copy.39), channel_id=2, replica_groups=mesh['seq'=2,'row'=4,'col'=4] {'row'}, dimensions={0}, use_global_device_ids=true | all-gather | bytes 337920 | tf_op jit(solution)/shard_map/all_gather | solution.py:88
  41.8 0.1 reshape.47
  42.1 0.3 convolution_bitcast_fusion
  42.4 0.3 fusion.16
  42.7 0.0 copy-start.1
  42.7 0.1 slice.8
  42.8 0.5 %reshape.46 = f32[8,8,1024]{2,1,0:T(8,128)S(1)} reshape(f32[8,8,32,32]{3,2,1,0:T(8,128)S(1)} %slice.8) | data formatting | bytes 524288 | tf_op jit(solution)/shard_map/reshape | solution.py:41
  43.3 0.0 copy-done
  43.3 0.1 copy-done.1
  43.4 1.1 %fusion.5 = bf16[8,8,128]{2,1,0:T(8,128)(2,1)} fusion(f32[8,8,1024]{2,1,0:T(8,128)S(1)} %reshape.46, f32[1024,128]{1,0:T(8,128)S(1)} %copy-done, bf16[8,8,128]{2,1,0:T(8,128)(2,1)S(1)} %copy-done.1, f32[8,8]{1,0:T(8,128)S(1)} %fusion.16), kind=kOutput, calls=%fused_computation.9 | convolution fusion | flops 100696064 | bytes 819456 | tf_op jit(solution)/shard_map/dot_general | solution.py:50
  (9 shorter events, 0.2 us)
Async XLA Ops:
  0.0 43.3 %copy-start = (f32[1024,128]{1,0:T(8,128)S(1)}, f32[1024,128]{1,0:T(8,128)}, u32[]{:S(2)}) copy-start(f32[1024,128]{1,0:T(8,128)} %param.18) | copy-start | bytes 1572868
  42.7 0.7 %copy-start.1 = (bf16[8,8,128]{2,1,0:T(8,128)(2,1)S(1)}, bf16[8,8,128]{2,1,0:T(8,128)(2,1)}, u32[]{:S(2)}) copy-start(bf16[8,8,128]{2,1,0:T(8,128)(2,1)} %param.19) | copy-start | bytes 49156
